TPU v7x, 32 devices: a whole 2x2x4 slice. The times are simulated.
32 devices in a mesh: ctx: 2 (over x), grp: 4 (over y, core), tp: 4 (over z).
Axes of the slice: x: 2, y: 2, z: 4, core: 2. Of those that a mesh axis runs over, the one named last changes fastest.
Arguments:
- tokens: bfloat16 [4096, 4608], P(('grp', 'ctx')), parts along dimension 0, may hold values from -6 to 6
- token_pos: int32 [4096], P(('grp', 'ctx')), parts along dimension 0, may hold values from 0 to 1023, as said below
- norm_gain: float32 [4608], replicated, may hold values from 0.1 to 1.9
- query_weight: bfloat16 [4608, 4096], P('ctx', 'tp'), may hold values from -0.09375 to 0.09375
- key_weight: bfloat16 [4608, 2048], P('ctx', 'tp'), may hold values from -0.09375 to 0.09375
- value_weight: bfloat16 [4608, 2048], P('ctx', 'tp'), may hold values from -0.09375 to 0.09375
Outputs:
- attended: bfloat16 [4096, 4096], P(('grp', 'ctx'), 'tp'), parts along dimension 0
There are 4 independent parts, one for each index of `grp`. A program takes and returns all parts, laid end to end along the dimension named above; an argument that names none is the same for every part. Nothing has to cross between parts.
Inputs may be any that keep to these rules, and one draw needn't show every extreme that they name: `token_pos`: the 512 rows of each index of ctx form two runs of 256 consecutive ascending positions, each starting at a multiple of 256; every position of the sequence occurs exactly once.
All inputs are finite; a program needn't handle non-finite values.
Results may differ from a plain program's by a relative error of at most 0.0077.
Values may be sent and summed in bfloat16 or wider, within the bound.
A program may use at most 128 MiB of HBM per device.

v0:
```python
import math

import jax
import jax.numpy as jnp
from jax import lax
from jax.sharding import PartitionSpec as P

HEAD_DIM = 128


query_scale = 144.0 ** (-0.5)


def rotate(field, positions):
    half = field.shape[-1] // 2
    freq = 10000.0 ** (-jnp.arange(half, dtype=jnp.float32) * 2.0 / field.shape[-1])
    angle = positions.astype(jnp.float32)[:, None] * freq[None, :]
    cosine = jnp.cos(angle)[:, None, :]
    sine = jnp.sin(angle)[:, None, :]
    first = field[..., :half]
    second = field[..., half:]
    return jnp.concatenate([first * cosine - second * sine, second * cosine + first * sine], -1)


def make_compute(query_run, pos_run, key_part, value_part, pos_part):

    def compute(state):
        numerator, total = state
        scores = jnp.einsum(
            "ngrd,mgd->grnm", query_run, key_part, preferred_element_type=jnp.float32
        )
        capped = 50.0 * jnp.tanh(scores / 50.0)
        allowed = pos_part[None, None, None, :] <= pos_run[None, None, :, None]
        weights = jnp.where(allowed, jnp.exp(capped), 0.0).astype(jnp.bfloat16)
        numerator = numerator + jnp.einsum(
            "grnm,mgd->ngrd", weights, value_part, preferred_element_type=jnp.float32
        )
        total = total + jnp.sum(weights.astype(jnp.float32), -1)
        return (numerator, total)

    return compute


def on_device(tokens, token_pos, norm_gain, query_weight, key_weight, value_weight):
    rows = tokens.shape[0]
    run_rows = rows // 2
    inputs = tokens.astype(jnp.float32)
    normed = (
        inputs
        * lax.rsqrt(jnp.mean(inputs * inputs, -1, keepdims=True) + 1e-06)
        * norm_gain[None, :]
    ).astype(jnp.bfloat16)

    def add_rows(piece):
        return jnp.dot(normed, piece, preferred_element_type=jnp.float32)

    query_sum = add_rows(lax.all_gather(query_weight, "ctx", axis=0, tiled=True))
    key_sum = add_rows(lax.all_gather(key_weight, "ctx", axis=0, tiled=True))
    value_sum = add_rows(lax.all_gather(value_weight, "ctx", axis=0, tiled=True))
    groups = key_weight.shape[1] // HEAD_DIM
    queries = rotate(query_sum.reshape(rows, 2 * groups, HEAD_DIM), token_pos) * query_scale
    queries = queries.astype(jnp.bfloat16).reshape(rows, groups, 2, HEAD_DIM)
    keys = (
        rotate(key_sum.reshape(rows, groups, HEAD_DIM), token_pos)
        .astype(jnp.bfloat16)
        .reshape(rows, groups * HEAD_DIM)
    )
    values = value_sum.astype(jnp.bfloat16)
    query_runs = [
        queries[run_index * run_rows : (run_index + 1) * run_rows] for run_index in range(2)
    ]
    pos_runs = [
        token_pos[run_index * run_rows : (run_index + 1) * run_rows] for run_index in range(2)
    ]
    run_initial = (
        jnp.zeros((run_rows, groups, 2, HEAD_DIM), jnp.float32),
        jnp.zeros((groups, 2, run_rows), jnp.float32),
    )
    initial = (run_initial, run_initial)
    key_rows = lax.all_gather(keys, "ctx", axis=0, tiled=True)
    value_rows = lax.all_gather(values, "ctx", axis=0, tiled=True)
    key_pos = lax.all_gather(token_pos, "ctx", axis=0, tiled=True)
    length = key_rows.shape[0]
    width = math.gcd(length, run_rows)

    def one_block(index, acc):
        key_part = lax.dynamic_slice_in_dim(key_rows, index * width, width, 0).reshape(
            width, groups, HEAD_DIM
        )
        value_part = lax.dynamic_slice_in_dim(value_rows, index * width, width, 0).reshape(
            width, groups, HEAD_DIM
        )
        pos_part = lax.dynamic_slice_in_dim(key_pos, index * width, width, 0)
        updated = []
        for run_index in range(2):
            compute = make_compute(
                query_runs[run_index], pos_runs[run_index], key_part, value_part, pos_part
            )
            state = compute(acc[run_index])
            updated.append(state)
        return (updated[0], updated[1])

    finished = lax.fori_loop(0, length // width, one_block, initial)
    numerator = jnp.concatenate([finished[0][0], finished[1][0]], 0)
    total = jnp.concatenate([finished[0][1], finished[1][1]], 2)
    attended = numerator / jnp.transpose(total, (2, 0, 1))[..., None]
    return attended.astype(jnp.bfloat16).reshape(rows, 2 * groups * HEAD_DIM)


def solution(mesh):
    in_specs = (
        P(("grp", "ctx"), None),
        P(("grp", "ctx")),
        P(),
        P("ctx", "tp"),
        P("ctx", "tp"),
        P("ctx", "tp"),
    )
    out_specs = P(("grp", "ctx"), "tp")
    return jax.shard_map(
        on_device, mesh=mesh, in_specs=in_specs, out_specs=out_specs, check_vma=False
    )
```

profile of v0, /device:TPU:0, one launch (start us, length us, event | category | flops | bytes accessed | tf_op | source)
XLA Modules:
  0.0 355.7 jit_solution(11255213720516889548)
XLA Ops:
  6.5 0.7 all-gather.11.cloned.1.call-update
  7.3 0.7 all-gather.7.cloned.1.call-update
  8.1 0.7 all-gather.15.cloned.1.call-update
  8.9 0.5 multiply_cosine_fusion
  9.7 5.3 %all-gather = s32[2,1,512]{2,1,0:T(1,128)S(1)} all-gather(s32[1,1,512]{2,1,0:T(1,128)S(1)} %bitcast.87), channel_id=1, replica_groups=mesh['ctx'=2,'grp'=4,'tp'=4] {'ctx'}, dimensions={0}, use_global_device_ids=true | all-gather | bytes 6144 | tf_op jit(solution)/shard_map/all_gather | solution.py:82
  15.0 3.3 fusion.4
  18.3 55.9 %all-gather.11.cloned.1.call-done = bf16[4608,512]{1,0:T(8,128)(2,1)} async-done(((bf16[2304,512]{1,0:T(8,128)(2,1)}), bf16[4608,512]{1,0:T(8,128)(2,1)}) %all-gather.11.cloned.1.call-update) | async-done | bytes 4718608 | tf_op jit(solution)/shard_map/all_gather | solution.py:58
  74.3 6.9 %fusion.10 = f32[512,512]{0,1:T(8,128)S(1)} fusion(bf16[4608,512]{1,0:T(8,128)(2,1)} %all-gather.11.cloned.1.call-done, bf16[512,4608]{1,0:T(8,128)(2,1)} %param.8, f32[4608]{0:T(1024)S(1)} %copy-done.4, f32[512]{0:T(512)S(1)} %add_rsqrt_fusion), kind=kOutput, calls=%fused_computation.37 | convolution fusion | flops 2425356288 | bytes 10506240 | tf_op jit(solution)/shard_map/dot_general | solution.py:55
  81.3 0.8 pad_maximum_fusion
  82.3 56.2 %all-gather.7.cloned.1.call-done = bf16[4608,512]{1,0:T(8,128)(2,1)} async-done(((bf16[2304,512]{1,0:T(8,128)(2,1)}), bf16[4608,512]{1,0:T(8,128)(2,1)}) %all-gather.7.cloned.1.call-update) | async-done | bytes 4718608 | tf_op jit(solution)/shard_map/all_gather | solution.py:59
  138.5 7.2 %convolution_convert_fusion = bf16[512,512]{1,0:T(8,128)(2,1)} fusion(bf16[4608,512]{1,0:T(8,128)(2,1)} %all-gather.7.cloned.1.call-done, bf16[512,4608]{1,0:T(8,128)(2,1)} %param.8, f32[4608]{0:T(1024)S(1)} %copy-done.4, f32[512]{0:T(512)S(1)} %add_rsqrt_fusion), kind=kOutput, calls=%fused_computation.28 | convolution fusion | flops 2425618432 | bytes 9981952 | tf_op jit(solution)/shard_map/dot_general | solution.py:55
  145.7 112.3 %all-gather.15.cloned.1.call-done = bf16[4608,1024]{1,0:T(8,128)(2,1)} async-done(((bf16[2304,1024]{1,0:T(8,128)(2,1)}), bf16[4608,1024]{1,0:T(8,128)(2,1)}) %all-gather.15.cloned.1.call-update) | async-done | bytes 9437200 | tf_op jit(solution)/shard_map/all_gather | solution.py:57
  258.0 9.1 %convolution_bitcast_fusion.2 = f32[64,8,8,128]{3,1,2,0:T(8,128)S(1)} fusion(bf16[4608,1024]{1,0:T(8,128)(2,1)} %all-gather.15.cloned.1.call-done, bf16[512,4608]{1,0:T(8,128)(2,1)} %param.8, f32[4608]{0:T(1024)S(1)} %copy-done.4, f32[512]{0:T(512)S(1)} %add_rsqrt_fusion), kind=kOutput, calls=%fused_computation.27 | convolution fusion | flops 4841275392 | bytes 16273408 | tf_op jit(solution)/shard_map/dot_general | solution.py:55
  267.1 0.5 copy.54
  267.6 1.1 multiply_subtract_fusion
  268.7 0.6 fusion.7
  269.4 0.9 copy.36
  270.3 0.9 copy.37
  271.2 9.6 %all-gather.13.cloned.1.call-done = bf16[1024,512]{0,1:T(8,128)(2,1)} async-done(((bf16[512,512]{0,1:T(8,128)(2,1)}), bf16[1024,512]{0,1:T(8,128)(2,1)}) %all-gather.13.cloned.1.call-update) | async-done | bytes 1048592 | tf_op jit(solution)/shard_map/all_gather | solution.py:80
  280.7 22.7 %all-gather.9.cloned.1.call-done = bf16[1024,512]{1,0:T(8,128)(2,1)} async-done(((bf16[512,512]{1,0:T(8,128)(2,1)}), bf16[1024,512]{1,0:T(8,128)(2,1)}) %all-gather.9.cloned.1.call-update) | async-done | bytes 1048592 | tf_op jit(solution)/shard_map/all_gather | solution.py:81
  303.5 33.7 %while.20 = (s32[]{:T(128)}, f32[256,4,2,128]{0,3,2,1:T(8,128)S(1)}, f32[4,2,256]{2,1,0:T(2,128)S(1)}, f32[256,4,2,128]{0,3,2,1:T(8,128)S(1)}, f32[4,2,256]{2,1,...) while((s32[]{:T(128)}, ...), condition=%wide.region_4.5_spmd.clone, body=%wide.region_1.4_spmd.clone.sunk | while | flops 544346112 | bytes 16586031 | solution.py:103
  303.7 1.0 constant_dynamic-slice_fusion.5
  304.7 2.0 convert_reduce_fusion.5
  306.7 1.7 constant_dynamic-slice_fusion.4
  308.4 1.1 copy.56
  309.9 0.5 copy-done.1
  310.6 0.9 convert_reduce_fusion.4
  312.1 1.0 constant_dynamic-slice_fusion.5
  313.1 2.0 convert_reduce_fusion.5
  315.1 1.7 constant_dynamic-slice_fusion.4
  316.8 1.1 copy.56
  318.3 0.5 copy-done.1
  319.0 0.9 convert_reduce_fusion.4
  320.6 1.0 constant_dynamic-slice_fusion.5
  321.5 2.0 convert_reduce_fusion.5
  323.6 1.7 constant_dynamic-slice_fusion.4
  325.2 1.1 copy.56
  326.7 0.5 copy-done.1
  327.5 0.9 convert_reduce_fusion.4
  329.0 1.0 constant_dynamic-slice_fusion.5
  330.0 2.0 convert_reduce_fusion.5
  332.0 1.7 constant_dynamic-slice_fusion.4
  333.7 1.1 copy.56
  335.2 0.5 copy-done.1
  335.9 0.9 convert_reduce_fusion.4
  337.6 4.0 %div.37 = f32[512,4,2,128]{3,2,1,0:T(2,128)} broadcast(f32[512,4,2]{2,1,0:T(4,128)S(1)} %copy.41), dimensions={0,1,2} | broadcast | bytes 2113536 | tf_op jit(solution)/shard_map/div | solution.py:106
  341.6 3.9 %div.38 = f32[512,1024]{1,0:T(8,128)} reshape(f32[512,4,2,128]{3,2,1,0:T(2,128)} %div.37) | data formatting | bytes 4194304 | tf_op jit(solution)/shard_map/div | solution.py:106
  346.2 3.0 fusion.8
  (67 shorter events, 6.6 us)
Async XLA Ops:
  6.5 67.7 %all-gather.11.cloned.1.call-start = ((), (), s32[]{:S(2)}) async-start(), calls=%async_computation.2 | async-start | bytes 7077888 | tf_op jit(solution)/shard_map/all_gather | solution.py:58
  7.3 131.2 %all-gather.7.cloned.1.call-start = ((), (), s32[]{:S(2)}) async-start(), calls=%async_computation | async-start | bytes 7077888 | tf_op jit(solution)/shard_map/all_gather | solution.py:59
  8.0 0.8 copy-start.3
  8.0 250.0 %all-gather.15.cloned.1.call-start = ((), (), s32[]{:S(2)}) async-start(), calls=%async_computation.4 | async-start | bytes 14155776 | tf_op jit(solution)/shard_map/all_gather | solution.py:57
  8.8 272.0 %all-gather.13.cloned.1.call-start = ((), (), s32[]{:S(2)}) async-start(), calls=%async_computation.3 | async-start | bytes 1572864 | tf_op jit(solution)/shard_map/all_gather | solution.py:80
  15.0 59.3 %copy-start.4 = (f32[4608]{0:T(1024)S(1)}, f32[4608]{0:T(1024)}, u32[]{:S(2)}) copy-start(f32[4608]{0:T(1024)} %param.10) | copy-start | bytes 55300
  82.2 221.3 %all-gather.9.cloned.1.call-start = ((), (), s32[]{:S(2)}) async-start(), calls=%async_computation.1 | async-start | bytes 1572864 | tf_op jit(solution)/shard_map/all_gather | solution.py:81
  304.7 2.0 copy-start
  309.5 1.0 copy-start.1
  309.5 1.1 copy-start.2
  313.1 2.0 copy-start
  317.9 1.0 copy-start.1
  317.9 1.1 copy-start.2
  321.5 2.0 copy-start
  326.3 1.0 copy-start.1
  326.3 1.1 copy-start.2
  330.0 2.0 copy-start
  334.8 1.0 copy-start.1
  334.8 1.1 copy-start.2
Sparse Core Ops, SparseCore 0:
  8.9 65.3 all-gather.10
  75.8 62.6 all-gather.6
  140.0 117.9 all-gather.14
  259.4 21.2 all-gather.12
  282.1 21.2 all-gather.8
where the time goes:
time: 356 us
  waiting for transfers between devices  259 us (73%)
  matrix products  37.8 us (11%)
  local copies, waits for them, and re-layouts  29.6 us (8%)
  between operations  13.3 us (4%)
  other arithmetic  10.3 us (3%)
  blocking collectives  5.29 us (1%)
    all_gather x1, waiting for transfers between devices, on_device(): lax.all_gather(query_weight, 'ctx', axis=0, tiled=True)  112 us
    all_gather x1, waiting for transfers between devices, on_device(): lax.all_gather(value_weight, 'ctx', axis=0, tiled=True)  56.2 us
    all_gather x1, waiting for transfers between devices, on_device(): key_sum = add_rows(lax.all_gather(key_weight, 'ctx', axis=0, tiled=True))  55.9 us
    dot_general x3, matrix products, add_rows(): return jnp.dot(normed, piece, preferred_element_type=jnp.float32)  23.2 us
    all_gather x1, waiting for transfers between devices, on_device(): value_rows = lax.all_gather(values, 'ctx', axis=0, tiled=True)  22.7 us
    dot_general x8, matrix products, compute(): jnp.einsum('ngrd,mgd->grnm', query_run, key_part, preferred_element_type=...  11.5 us
    dynamic_slice x8, local copies, waits for them, and re-layouts, one_block(): lax.dynamic_slice_in_dim(value_rows, index * width, width, 0)  11 us
    all_gather x1, waiting for transfers between devices, on_device(): key_rows = lax.all_gather(keys, 'ctx', axis=0, tiled=True)  9.57 us
  transfers between devices with their start and end apart: 5, of which 5 were waited for; matrix products, arithmetic and copies ran while one was open for 9% of the time, Pallas kernels for 0%

commit v1 on v0

v1 whole, which is shorter than its diff:
```python
import functools
import math

import jax
import jax.numpy as jnp
from jax import lax
from jax.experimental import pallas as pl
from jax.experimental.pallas import tpu as pltpu
from jax.sharding import PartitionSpec as P

HEAD_DIM = 128
BLOCK = 2 * HEAD_DIM
MESH = pl.DeviceIdType.MESH

query_scale = 144.0 ** (-0.5)


def each(start, stop, body):
    if stop - start == 1:
        body(start)
    elif stop > start:
        lax.fori_loop(start, stop, lambda i, _: (body(i), None)[1], None)


def kernel(
    n, grp, pos_ref, freq_ref, gain_ref, tok_ref, q_ref, k_ref, v_ref, out_ref,
    wbuf, normed, kvbuf, posbuf, qbuf, acc, cos_ref, sin_ref, qpos_ref,
    tok_sem, own_sem, x_send, x_recv, y_send, y_recv, s_send, s_recv, t_send, t_recv,
    kv_send, kv_recv, pos_send, pos_recv,
):
    c = lax.axis_index("ctx")
    g = lax.axis_index("grp")
    pairs = grp // 2
    near = g % 2
    pair = g // 2
    sibling = pair * 2 + (1 - near)
    depth = q_ref.shape[0]
    part = depth // grp
    rows = tok_ref.shape[0]
    kv_blocks = k_ref.shape[1] // BLOCK
    q_blocks = q_ref.shape[1] // BLOCK
    sources = [(k_ref, i) for i in range(kv_blocks)]
    sources += [(v_ref, i) for i in range(kv_blocks)]
    sources += [(q_ref, i) for i in range(q_blocks)]
    blocks = len(sources)

    def region(owner, member):
        return pl.ds(pl.multiple_of(owner * depth + member * part, 16), part)

    def peer(d):
        return lax.rem(c + d, n)

    def source(d):
        return lax.rem(c + n - d, n)

    def far(j):
        return lax.rem(pair + j, pairs)

    def near_of(j):
        return lax.rem(pair + pairs - j, pairs)

    def x_copy(b, d):
        ref, col = sources[b]
        return pltpu.make_async_remote_copy(
            src_ref=ref.at[pl.ds(pl.multiple_of(g * part, 16), part), pl.ds(col * BLOCK, BLOCK)],
            dst_ref=wbuf.at[b, region(c, g)],
            send_sem=x_send.at[b, d - 1], recv_sem=x_recv.at[b, d - 1],
            device_id={"ctx": peer(d)}, device_id_type=MESH,
        )

    def hop(b, where, send, recv, member):
        return pltpu.make_async_remote_copy(
            src_ref=wbuf.at[b, where], dst_ref=wbuf.at[b, where],
            send_sem=send, recv_sem=recv, device_id={"grp": member}, device_id_type=MESH,
        )

    def y_copy(b, d, j):
        return hop(b, region(source(d), g), y_send.at[b, d - 1, j - 1], y_recv.at[b, d - 1, j - 1],
                   far(j) * 2 + near)

    def y_wait(b, d, j):
        hop(b, region(source(d), near_of(j) * 2 + near), y_send.at[b, d - 1, j - 1],
            y_recv.at[b, d - 1, j - 1], sibling).wait_recv()

    def s_copy(b, d):
        return hop(b, region(source(d), g), s_send.at[b, d - 1], s_recv.at[b, d - 1], sibling)

    def s_wait(b, d):
        hop(b, region(source(d), sibling), s_send.at[b, d - 1], s_recv.at[b, d - 1],
            sibling).wait_recv()

    def t_copy(b, d, j):
        return hop(b, region(source(d), near_of(j) * 2 + near), t_send.at[b, d - 1, j - 1],
                   t_recv.at[b, d - 1, j - 1], sibling)

    def t_wait(b, d, j):
        hop(b, region(source(d), near_of(j) * 2 + 1 - near), t_send.at[b, d - 1, j - 1],
            t_recv.at[b, d - 1, j - 1], sibling).wait_recv()

    def kv_copy(b, d, owner):
        return pltpu.make_async_remote_copy(
            src_ref=kvbuf.at[b, owner], dst_ref=kvbuf.at[b, owner],
            send_sem=kv_send.at[b, d - 1], recv_sem=kv_recv.at[b, d - 1],
            device_id={"ctx": peer(d)}, device_id_type=MESH,
        )

    def pos_copy(d, owner):
        return pltpu.make_async_remote_copy(
            src_ref=pos_ref, dst_ref=posbuf.at[owner],
            send_sem=pos_send.at[d - 1], recv_sem=pos_recv.at[d - 1],
            device_id={"ctx": peer(d)}, device_id_type=MESH,
        )

    def own_copy(b):
        ref, col = sources[b]
        return pltpu.make_async_copy(
            ref.at[:, pl.ds(col * BLOCK, BLOCK)],
            wbuf.at[b, pl.ds(pl.multiple_of(c * depth, 16), depth)], own_sem.at[b],
        )

    tok_copy = pltpu.make_async_copy(tok_ref, normed, tok_sem)
    tok_copy.start()

    barrier = pltpu.get_barrier_semaphore()

    def greet(**where):
        pl.semaphore_signal(barrier, inc=1, device_id=where, device_id_type=MESH)

    each(1, n, lambda d: greet(ctx=peer(d)))
    each(1, pairs, lambda j: greet(grp=far(j) * 2 + near))
    greet(grp=sibling)
    pl.semaphore_wait(barrier, n - 1 + pairs - 1 + 1)

    def send_block(b):
        each(1, n, lambda d: x_copy(b, d).start())

    send_block(0)
    each(1, n, lambda d: pos_copy(d, c).start())
    send_block(1)
    for b in range(blocks):
        own_copy(b).start()

    posbuf[c] = pos_ref[...]
    qpos = jnp.transpose(
        jnp.broadcast_to(pos_ref[0:1, :].astype(jnp.float32), (HEAD_DIM, rows)), (1, 0)
    )
    qpos_ref[...] = qpos
    angle = qpos * freq_ref[...]
    lane = lax.broadcasted_iota(jnp.int32, angle.shape, 1)
    sine = jnp.sin(angle)
    cos_ref[...] = jnp.cos(angle)
    sin_ref[...] = jnp.where(lane < HEAD_DIM // 2, -sine, sine)

    tok_copy.wait()
    strip = 32

    def norm_rows(i):
        where = pl.ds(pl.multiple_of(i * strip, strip), strip)
        inputs = normed[where, :].astype(jnp.float32)
        mean = jnp.mean(inputs * inputs, -1, keepdims=True)
        normed[where, :] = (inputs * lax.rsqrt(mean + 1e-06) * gain_ref[...]).astype(jnp.bfloat16)

    each(0, rows // strip, norm_rows)

    tall = math.gcd(rows, 256)

    def project(b, target, rope, scale):
        def tile(i):
            where = pl.ds(pl.multiple_of(i * tall, tall), tall)
            field = jnp.dot(normed[where, :], wbuf[b], preferred_element_type=jnp.float32)
            if rope:
                cosine, sine = cos_ref[where, :], sin_ref[where, :]
                halves = []
                for h in range(2):
                    one = field[:, h * HEAD_DIM : (h + 1) * HEAD_DIM]
                    halves.append(one * cosine + pltpu.roll(one, HEAD_DIM // 2, 1) * sine)
                field = jnp.concatenate(halves, -1)
            if scale is not None:
                field = field * scale
            target[where, :] = field.astype(jnp.bfloat16)

        each(0, rows // tall, tile)

    def attend(b, owner, first, last):
        piece, col = b // 2, (b % 2) * HEAD_DIM

        def tile(i):
            where = pl.ds(pl.multiple_of(i * tall, tall), tall)
            keys = kvbuf[piece, owner, :, pl.ds(col, HEAD_DIM)]
            values = kvbuf[kv_blocks + piece, owner, :, pl.ds(col, HEAD_DIM)]
            values = jnp.concatenate([values, jnp.ones_like(values)], -1)
            key_pos = posbuf[owner, 0:1, :].astype(jnp.float32)
            allowed = key_pos <= qpos_ref[where, 0:1]
            for h in range(2):
                cols = pl.ds(h * HEAD_DIM, HEAD_DIM)
                scores = lax.dot_general(
                    qbuf[b, where, cols], keys, (((1,), (1,)), ((), ())),
                    preferred_element_type=jnp.float32,
                )
                capped = jnp.tanh(scores * (1.0 / 50.0)) * (50.0 * math.log2(math.e))
                weights = jnp.where(allowed, jnp.exp2(capped), 0.0).astype(jnp.bfloat16)
                both = jnp.dot(weights, values, preferred_element_type=jnp.float32)
                if not first:
                    both = both + acc[b, h, where, :]
                if last:
                    done = both[:, :HEAD_DIM] / both[:, HEAD_DIM:]
                    out_ref[where, pl.ds(b * BLOCK + h * HEAD_DIM, HEAD_DIM)] = done.astype(
                        out_ref.dtype
                    )
                else:
                    acc[b, h, where, :] = both

        each(0, rows // tall, tile)

    received = set()

    def attend_others(b):
        piece = b // 2
        if "pos" not in received:
            received.add("pos")
            each(1, n, lambda d: pos_copy(d, source(d)).wait_recv())
        for index in (piece, kv_blocks + piece):
            if index not in received:
                received.add(index)
                each(1, n, lambda d: kv_copy(index, d, source(d)).wait_recv())
        each(1, n - 1, lambda d: attend(b, source(d), False, False))
        attend(b, source(n - 1), False, True)

    def send_kv(b):
        each(1, n, lambda d: kv_copy(b, d, c).start())

    for t in range(blocks + 2):
        if t < blocks:
            def forward(d, b=t):
                x_copy(b, d).wait_recv()
                each(1, pairs, lambda j: y_copy(b, d, j).start())
                s_copy(b, d).start()

            each(1, n, forward)
        if 1 <= t <= blocks:
            def onward(d, b=t - 1):
                def one(j):
                    y_wait(b, d, j)
                    t_copy(b, d, j).start()

                each(1, pairs, one)

            each(1, n, onward)
        if t >= 2:
            b = t - 2

            def arrive(d, b=b):
                s_wait(b, d)
                each(1, pairs, lambda j: t_wait(b, d, j))

            each(1, n, arrive)
            own_copy(b).wait()
            if b < 2 * kv_blocks:
                project(b, kvbuf.at[b, c], b < kv_blocks, None)
        if 3 <= t <= 2 * kv_blocks + 2:
            send_kv(t - 3)
        if t + 2 < blocks:
            send_block(t + 2)
        if t >= 2 and t - 2 >= 2 * kv_blocks:
            h = t - 2 - 2 * kv_blocks
            project(t - 2, qbuf.at[h], True, query_scale)
            attend(h, c, True, False)
            if h > 0:
                attend_others(h - 1)
    attend_others(q_blocks - 1)

    def settle(d):
        pos_copy(d, c).wait_send()
        for b in range(2 * kv_blocks):
            kv_copy(b, d, c).wait_send()
        for b in range(blocks):
            x_copy(b, d).wait_send()
            s_copy(b, d).wait_send()

            def pair_sends(j, b=b):
                y_copy(b, d, j).wait_send()
                t_copy(b, d, j).wait_send()

            each(1, pairs, pair_sends)

    each(1, n, settle)


def on_device(n, grp, tokens, token_pos, norm_gain, query_weight, key_weight, value_weight):
    rows, width = tokens.shape
    depth, q_cols = query_weight.shape
    kv_cols = key_weight.shape[1]
    q_blocks, kv_blocks = q_cols // BLOCK, kv_cols // BLOCK
    blocks = q_blocks + 2 * kv_blocks
    pairs = grp // 2
    half = HEAD_DIM // 2
    freq = 10000.0 ** (-jnp.arange(half, dtype=jnp.float32) * 2.0 / HEAD_DIM)
    freq = jnp.concatenate([freq, freq])[None, :]
    pos = jnp.broadcast_to(token_pos[None, :], (8, rows))
    dma = pltpu.SemaphoreType.DMA
    far = max(pairs - 1, 1)
    vmem = pl.BlockSpec(memory_space=pltpu.VMEM)
    anywhere = pl.BlockSpec(memory_space=pl.ANY)
    return pl.pallas_call(
        functools.partial(kernel, n, grp),
        out_shape=jax.ShapeDtypeStruct((rows, q_cols), jnp.bfloat16),
        in_specs=[vmem] * 3 + [anywhere] * 4,
        out_specs=vmem,
        scratch_shapes=[
            pltpu.VMEM((blocks, n * depth, BLOCK), jnp.bfloat16),
            pltpu.VMEM((rows, width), jnp.bfloat16),
            pltpu.VMEM((2 * kv_blocks, n, rows, BLOCK), jnp.bfloat16),
            pltpu.VMEM((n, 8, rows), jnp.int32),
            pltpu.VMEM((q_blocks, rows, BLOCK), jnp.bfloat16),
            pltpu.VMEM((q_blocks, 2, rows, BLOCK), jnp.float32),
            pltpu.VMEM((rows, HEAD_DIM), jnp.float32),
            pltpu.VMEM((rows, HEAD_DIM), jnp.float32),
            pltpu.VMEM((rows, HEAD_DIM), jnp.float32),
            dma(()),
            dma((blocks,)),
            dma((blocks, n - 1)),
            dma((blocks, n - 1)),
            dma((blocks, n - 1, far)),
            dma((blocks, n - 1, far)),
            dma((blocks, n - 1)),
            dma((blocks, n - 1)),
            dma((blocks, n - 1, far)),
            dma((blocks, n - 1, far)),
            dma((2 * kv_blocks, n - 1)),
            dma((2 * kv_blocks, n - 1)),
            dma((n - 1,)),
            dma((n - 1,)),
        ],
        compiler_params=pltpu.CompilerParams(
            collective_id=0, has_side_effects=True, vmem_limit_bytes=64 * 1024 * 1024 - 65536
        ),
    )(pos, freq, norm_gain[None, :], tokens, query_weight, key_weight, value_weight)


def solution(mesh):
    in_specs = (
        P(("grp", "ctx"), None),
        P(("grp", "ctx")),
        P(),
        P("ctx", "tp"),
        P("ctx", "tp"),
        P("ctx", "tp"),
    )
    out_specs = P(("grp", "ctx"), "tp")
    return jax.shard_map(
        functools.partial(on_device, mesh.shape["ctx"], mesh.shape["grp"]),
        mesh=mesh, in_specs=in_specs, out_specs=out_specs, check_vma=False,
    )
```

time: 356 us -> 97.8 us (0.27)
  waiting for transfers between devices: 259 us -> 0 us
  Pallas kernels: 0 us -> 92 us
  matrix products: 37.8 us -> 0 us
  local copies, waits for them, and re-layouts: 29.6 us -> 4.89 us
  between operations: 13.3 us -> 0.01 us
  other arithmetic: 10.3 us -> 0.6 us
  blocking collectives: 5.29 us -> 0 us
    all_gather x5 -> x0, waiting for transfers between devices: 257 us -> none  [the longest x1 112 us: on_device(): lax.all_gather(query_weight, 'ctx', axis=0, tiled=True)]
    pallas_call x0 -> x1, Pallas kernels: none -> 92 us  [on_device(): pl.pallas_call(functools.partial(kernel, n, grp), out_shape=jax.ShapeDtyp...]
    dot_general x19 -> x0, matrix products: 37.8 us -> none  [the longest x3 23.2 us: add_rows(): return jnp.dot(normed, piece, preferred_element_type=jnp.float32)]
    dynamic_slice x16 -> x0, local copies, waits for them, and re-layouts: 15.2 us -> none  [the longest x8 11 us: one_block(): lax.dynamic_slice_in_dim(value_rows, index * width, width, 0)]
    div x2 -> x0, local copies, waits for them, and re-layouts: 7.89 us -> none  [on_device(): attended = numerator / jnp.transpose(total, (2, 0, 1))[..., None]]
    all_gather x1 -> x0, blocking collectives: 5.29 us -> none  [on_device(): key_pos = lax.all_gather(token_pos, 'ctx', axis=0, tiled=True)]
    convert_element_type x3 -> x0, other arithmetic: 3.57 us -> none  [the longest x1 2.95 us: on_device(): return attended.astype(jnp.bfloat16).reshape(rows, 2 * groups * HEAD_DIM)]
  transfers between devices with their start and end apart: 5 -> 0, of which waited for: 5 -> 0; matrix products, arithmetic and copies ran while one was open for 9% -> 0% of each run, Pallas kernels for 0% -> 0%
where the time goes in v1:
time: 97.8 us; the launch traced here: 97.5 us
  Pallas kernels  92 us (94%)
  local copies, waits for them, and re-layouts  4.89 us (5%)
    pallas_call x1, Pallas kernels, on_device(): pl.pallas_call(functools.partial(kernel, n, grp), out_shape=jax.ShapeDtyp...  92 us
    unnamed x1, local copies, waits for them, and re-layouts  2.26 us

profile of v1, /device:TPU:0, one launch (start us, length us, event | category | flops | bytes accessed | tf_op | source)
XLA Modules:
  0.0 97.5 jit_solution(6725185464663181037)
XLA Ops:
  0.0 0.6 maximum_bitcast_fusion.freq_ref
  0.6 1.3 %broadcast_in_dim.12.pos_ref = s32[8,512]{1,0:T(8,128)} broadcast(s32[512]{0:T(512)} %param.7), dimensions={1} | broadcast | bytes 18432 | tf_op jit(solution)/shard_map/broadcast_in_dim | solution.py:299
  1.9 1.3 %broadcast_in_dim.14.gain_ref = f32[1,4608]{1,0:T(1,128)} reshape(f32[4608]{0:T(1024)} %param.8) | data formatting | bytes 36864 | tf_op jit(solution)/shard_map/broadcast_in_dim | solution.py:337
  3.2 92.0 %shard_map.64 = bf16[512,1024]{1,0:T(8,128)(2,1)} custom-call(s32[8,512]{1,0:T(8,128)} %broadcast_in_dim.12.pos_ref, f32[1,128]{1,0:T(1,128)} %maximum_bitcast_fusion.freq_ref, f32[1,4608]{1,0:T(1,128)} %broadcast_in_dim.14.gain_ref, bf16[512,4608]{1,0:T(8,128)(2,1)} %tok_ref.1, bf16[2304,1024]{1,0:T(8,128)(2,1)} %q_ref.1, bf16[2304,512]{1,0:T(8,128)(2,1)} %k_ref.1, ...), custom_call_target="tpu_custom_call" | custom-call | tf_op jit(solution)/shard_map/pallas_call | solution.py:304
  95.3 2.3 %copy.8 = bf16[512,1024]{1,0:T(8,128)(2,1)} copy(bf16[512,1024]{1,0:T(8,128)(2,1)} %shard_map.64) | data formatting | bytes 2097152
  (1 shorter events, 0.0 us)

commit v2 on v1

--- a/solution.py
+++ b/solution.py
@@ -3,6 +3,7 @@
 
 import jax
 import jax.numpy as jnp
+import numpy as np
 from jax import lax
 from jax.experimental import pallas as pl
 from jax.experimental.pallas import tpu as pltpu
@@ -38,6 +39,7 @@
     part = depth // grp
     rows = tok_ref.shape[0]
     kv_blocks = k_ref.shape[1] // BLOCK
+    groups = k_ref.shape[1] // HEAD_DIM
     q_blocks = q_ref.shape[1] // BLOCK
     sources = [(k_ref, i) for i in range(kv_blocks)]
     sources += [(v_ref, i) for i in range(kv_blocks)]
@@ -106,7 +108,7 @@
 
     def pos_copy(d, owner):
         return pltpu.make_async_remote_copy(
-            src_ref=pos_ref, dst_ref=posbuf.at[owner],
+            src_ref=posbuf.at[owner], dst_ref=posbuf.at[owner],
             send_sem=pos_send.at[d - 1], recv_sem=pos_recv.at[d - 1],
             device_id={"ctx": peer(d)}, device_id_type=MESH,
         )
@@ -135,14 +137,14 @@
         each(1, n, lambda d: x_copy(b, d).start())
 
     send_block(0)
-    each(1, n, lambda d: pos_copy(d, c).start())
     send_block(1)
     for b in range(blocks):
         own_copy(b).start()
 
-    posbuf[c] = pos_ref[...]
+    lanes = pos_ref[...][None, :]
+    posbuf[c] = jnp.broadcast_to(lanes, posbuf.shape[1:])
     qpos = jnp.transpose(
-        jnp.broadcast_to(pos_ref[0:1, :].astype(jnp.float32), (HEAD_DIM, rows)), (1, 0)
+        jnp.broadcast_to(lanes.astype(jnp.float32), (HEAD_DIM, rows)), (1, 0)
     )
     qpos_ref[...] = qpos
     angle = qpos * freq_ref[...]
@@ -158,13 +160,13 @@
         where = pl.ds(pl.multiple_of(i * strip, strip), strip)
         inputs = normed[where, :].astype(jnp.float32)
         mean = jnp.mean(inputs * inputs, -1, keepdims=True)
-        normed[where, :] = (inputs * lax.rsqrt(mean + 1e-06) * gain_ref[...]).astype(jnp.bfloat16)
+        normed[where, :] = (inputs * lax.rsqrt(mean + 1e-06) * gain_ref[...][None, :]).astype(jnp.bfloat16)
 
     each(0, rows // strip, norm_rows)
 
     tall = math.gcd(rows, 256)
 
-    def project(b, target, rope, scale):
+    def project(b, store, rope, scale):
         def tile(i):
             where = pl.ds(pl.multiple_of(i * tall, tall), tall)
             field = jnp.dot(normed[where, :], wbuf[b], preferred_element_type=jnp.float32)
@@ -177,17 +179,15 @@
                 field = jnp.concatenate(halves, -1)
             if scale is not None:
                 field = field * scale
-            target[where, :] = field.astype(jnp.bfloat16)
+            store(where, field.astype(jnp.bfloat16))
 
         each(0, rows // tall, tile)
 
     def attend(b, owner, first, last):
-        piece, col = b // 2, (b % 2) * HEAD_DIM
-
         def tile(i):
             where = pl.ds(pl.multiple_of(i * tall, tall), tall)
-            keys = kvbuf[piece, owner, :, pl.ds(col, HEAD_DIM)]
-            values = kvbuf[kv_blocks + piece, owner, :, pl.ds(col, HEAD_DIM)]
+            keys = kvbuf[b, owner]
+            values = kvbuf[groups + b, owner]
             values = jnp.concatenate([values, jnp.ones_like(values)], -1)
             key_pos = posbuf[owner, 0:1, :].astype(jnp.float32)
             allowed = key_pos <= qpos_ref[where, 0:1]
@@ -215,19 +215,32 @@
     received = set()
 
     def attend_others(b):
-        piece = b // 2
         if "pos" not in received:
             received.add("pos")
             each(1, n, lambda d: pos_copy(d, source(d)).wait_recv())
-        for index in (piece, kv_blocks + piece):
+        for index in (b, groups + b):
             if index not in received:
                 received.add(index)
                 each(1, n, lambda d: kv_copy(index, d, source(d)).wait_recv())
         each(1, n - 1, lambda d: attend(b, source(d), False, False))
         attend(b, source(n - 1), False, True)
 
-    def send_kv(b):
-        each(1, n, lambda d: kv_copy(b, d, c).start())
+    def send_group(h):
+        each(1, n, lambda d: kv_copy(h, d, c).start())
+        each(1, n, lambda d: kv_copy(groups + h, d, c).start())
+
+    def store_kv(first):
+        def store(where, field):
+            kvbuf[first, c, where, :] = field[:, :HEAD_DIM]
+            kvbuf[first + 1, c, where, :] = field[:, HEAD_DIM:]
+
+        return store
+
+    def store_q(h):
+        def store(where, field):
+            qbuf[h, where, :] = field
+
+        return store
 
     for t in range(blocks + 2):
         if t < blocks:
@@ -256,22 +269,27 @@
             each(1, n, arrive)
             own_copy(b).wait()
             if b < 2 * kv_blocks:
-                project(b, kvbuf.at[b, c], b < kv_blocks, None)
-        if 3 <= t <= 2 * kv_blocks + 2:
-            send_kv(t - 3)
+                project(b, store_kv(2 * b), b < kv_blocks, None)
         if t + 2 < blocks:
             send_block(t + 2)
+        if t == 2:
+            each(1, n, lambda d: pos_copy(d, c).start())
+        if t >= blocks - 2:
+            share = [h for h in range(groups) if min(blocks - 2 + h, blocks) == t]
+            for h in share:
+                send_group(h)
         if t >= 2 and t - 2 >= 2 * kv_blocks:
             h = t - 2 - 2 * kv_blocks
-            project(t - 2, qbuf.at[h], True, query_scale)
+            project(t - 2, store_q(h), True, query_scale)
             attend(h, c, True, False)
-            if h > 0:
-                attend_others(h - 1)
-    attend_others(q_blocks - 1)
+            if t == blocks:
+                attend_others(0)
+    for h in range(1, q_blocks):
+        attend_others(h)
 
     def settle(d):
         pos_copy(d, c).wait_send()
-        for b in range(2 * kv_blocks):
+        for b in range(2 * groups):
             kv_copy(b, d, c).wait_send()
         for b in range(blocks):
             x_copy(b, d).wait_send()
@@ -294,9 +312,8 @@
     blocks = q_blocks + 2 * kv_blocks
     pairs = grp // 2
     half = HEAD_DIM // 2
-    freq = 10000.0 ** (-jnp.arange(half, dtype=jnp.float32) * 2.0 / HEAD_DIM)
-    freq = jnp.concatenate([freq, freq])[None, :]
-    pos = jnp.broadcast_to(token_pos[None, :], (8, rows))
+    freq = 10000.0 ** (-np.arange(half) * 2.0 / HEAD_DIM)
+    freq = np.concatenate([freq, freq])[None, :].astype(np.float32)
     dma = pltpu.SemaphoreType.DMA
     far = max(pairs - 1, 1)
     vmem = pl.BlockSpec(memory_space=pltpu.VMEM)
@@ -309,7 +326,7 @@
         scratch_shapes=[
             pltpu.VMEM((blocks, n * depth, BLOCK), jnp.bfloat16),
             pltpu.VMEM((rows, width), jnp.bfloat16),
-            pltpu.VMEM((2 * kv_blocks, n, rows, BLOCK), jnp.bfloat16),
+            pltpu.VMEM((4 * kv_blocks, n, rows, HEAD_DIM), jnp.bfloat16),
             pltpu.VMEM((n, 8, rows), jnp.int32),
             pltpu.VMEM((q_blocks, rows, BLOCK), jnp.bfloat16),
             pltpu.VMEM((q_blocks, 2, rows, BLOCK), jnp.float32),
@@ -326,15 +343,15 @@
             dma((blocks, n - 1)),
             dma((blocks, n - 1, far)),
             dma((blocks, n - 1, far)),
-            dma((2 * kv_blocks, n - 1)),
-            dma((2 * kv_blocks, n - 1)),
+            dma((4 * kv_blocks, n - 1)),
+            dma((4 * kv_blocks, n - 1)),
             dma((n - 1,)),
             dma((n - 1,)),
         ],
         compiler_params=pltpu.CompilerParams(
             collective_id=0, has_side_effects=True, vmem_limit_bytes=64 * 1024 * 1024 - 65536
         ),
-    )(pos, freq, norm_gain[None, :], tokens, query_weight, key_weight, value_weight)
+    )(token_pos, freq, norm_gain, tokens, query_weight, key_weight, value_weight)
 
 
 def solution(mesh):

time: 97.8 us -> 84.7 us (0.87)
  Pallas kernels: 92 us -> 82.3 us
  local copies, waits for them, and re-layouts: 4.89 us -> 2.26 us
    pallas_call x1, Pallas kernels: 92 us -> 82.3 us  [on_device(): pl.pallas_call(functools.partial(kernel, n, grp), out_shape=jax.ShapeDtyp...]
    broadcast_in_dim x2 -> x0, local copies, waits for them, and re-layouts: 2.63 us -> none  [the longest x1 1.35 us: on_device(): norm_gain[None, :]]
where the time goes in v2:
time: 84.7 us; the launch traced here: 84.5 us
  Pallas kernels  82.3 us (97%)
  local copies, waits for them, and re-layouts  2.26 us (3%)
    pallas_call x1, Pallas kernels, on_device(): pl.pallas_call(functools.partial(kernel, n, grp), out_shape=jax.ShapeDtyp...  82.3 us
    unnamed x1, local copies, waits for them, and re-layouts  2.26 us

profile of v2, /device:TPU:0, one launch (start us, length us, event | category | flops | bytes accessed | tf_op | source)
XLA Modules:
  0.0 84.5 jit_solution(17318339072330711148)
XLA Ops:
  0.0 82.3 %shard_map.73 = bf16[512,1024]{1,0:T(8,128)(2,1)} custom-call(s32[512]{0:T(512)} %pos_ref.1, f32[1,128]{1,0:T(1,128)} %constant.2.clone.freq_ref, f32[4608]{0:T(1024)} %gain_ref.1, bf16[512,4608]{1,0:T(8,128)(2,1)} %tok_ref.1, bf16[2304,1024]{1,0:T(8,128)(2,1)} %q_ref.1, bf16[2304,512]{1,0:T(8,128)(2,1)} %k_ref.1, bf16[2304,512]{1,0:T(8,128)(2,1)} %v_ref.1), custom_call_target="tpu_custom_call" | custom-call | tf_op jit(solution)/shard_map/pallas_call | solution.py:321
  82.3 2.3 %copy.9 = bf16[512,1024]{1,0:T(8,128)(2,1)} copy(bf16[512,1024]{1,0:T(8,128)(2,1)} %shard_map.73) | data formatting | bytes 2097152

commit v3 on v2

--- a/solution.py
+++ b/solution.py
@@ -62,10 +62,8 @@
         return lax.rem(pair + pairs - j, pairs)
 
     def x_copy(b, d):
-        ref, col = sources[b]
         return pltpu.make_async_remote_copy(
-            src_ref=ref.at[pl.ds(pl.multiple_of(g * part, 16), part), pl.ds(col * BLOCK, BLOCK)],
-            dst_ref=wbuf.at[b, region(c, g)],
+            src_ref=wbuf.at[b, region(c, g)], dst_ref=wbuf.at[b, region(c, g)],
             send_sem=x_send.at[b, d - 1], recv_sem=x_recv.at[b, d - 1],
             device_id={"ctx": peer(d)}, device_id_type=MESH,
         )
@@ -121,7 +119,11 @@
         )
 
     tok_copy = pltpu.make_async_copy(tok_ref, normed, tok_sem)
+    own_copy(0).start()
+    own_copy(1).start()
     tok_copy.start()
+    for b in range(2, blocks):
+        own_copy(b).start()
 
     barrier = pltpu.get_barrier_semaphore()
 
@@ -134,12 +136,11 @@
     pl.semaphore_wait(barrier, n - 1 + pairs - 1 + 1)
 
     def send_block(b):
+        own_copy(b).wait()
         each(1, n, lambda d: x_copy(b, d).start())
 
     send_block(0)
     send_block(1)
-    for b in range(blocks):
-        own_copy(b).start()
 
     lanes = pos_ref[...][None, :]
     posbuf[c] = jnp.broadcast_to(lanes, posbuf.shape[1:])
@@ -267,7 +268,6 @@
                 each(1, pairs, lambda j: t_wait(b, d, j))
 
             each(1, n, arrive)
-            own_copy(b).wait()
             if b < 2 * kv_blocks:
                 project(b, store_kv(2 * b), b < kv_blocks, None)
         if t + 2 < blocks:
@@ -304,6 +304,12 @@
     each(1, n, settle)
 
 
+def write_out(in_ref, out_ref, sem):
+    copy = pltpu.make_async_copy(in_ref, out_ref, sem)
+    copy.start()
+    copy.wait()
+
+
 def on_device(n, grp, tokens, token_pos, norm_gain, query_weight, key_weight, value_weight):
     rows, width = tokens.shape
     depth, q_cols = query_weight.shape
@@ -318,10 +324,11 @@
     far = max(pairs - 1, 1)
     vmem = pl.BlockSpec(memory_space=pltpu.VMEM)
     anywhere = pl.BlockSpec(memory_space=pl.ANY)
-    return pl.pallas_call(
+    held = [pltpu.with_memory_space_constraint(x, pltpu.HBM) for x in (tokens, query_weight, key_weight, value_weight)]
+    attended = pl.pallas_call(
         functools.partial(kernel, n, grp),
-        out_shape=jax.ShapeDtypeStruct((rows, q_cols), jnp.bfloat16),
-        in_specs=[vmem] * 3 + [anywhere] * 4,
+        out_shape=pltpu.VMEM((rows, q_cols), jnp.bfloat16),
+        in_specs=[vmem] * 3 + [pl.BlockSpec(memory_space=pltpu.HBM)] * 4,
         out_specs=vmem,
         scratch_shapes=[
             pltpu.VMEM((blocks, n * depth, BLOCK), jnp.bfloat16),
@@ -349,9 +356,17 @@
             dma((n - 1,)),
         ],
         compiler_params=pltpu.CompilerParams(
-            collective_id=0, has_side_effects=True, vmem_limit_bytes=64 * 1024 * 1024 - 65536
+            collective_id=0, has_side_effects=True, vmem_limit_bytes=44 * 1024 * 1024
         ),
-    )(token_pos, freq, norm_gain, tokens, query_weight, key_weight, value_weight)
+    )(token_pos, freq, norm_gain, *held)
+    return pl.pallas_call(
+        write_out,
+        out_shape=jax.ShapeDtypeStruct(attended.shape, attended.dtype),
+        in_specs=[vmem],
+        out_specs=anywhere,
+        scratch_shapes=[dma(())],
+        compiler_params=pltpu.CompilerParams(vmem_limit_bytes=4 * 1024 * 1024),
+    )(attended)
 
 
 def solution(mesh):

time: 84.7 us -> 83.6 us (0.987)
  Pallas kernels: 82.3 us -> 81.3 us
    pallas_call x1 -> x2, Pallas kernels: 82.3 us -> 81.3 us  [the longest x1 80.3 us: on_device(): pl.pallas_call(functools.partial(kernel, n, grp), out_shape=pltpu.VMEM((r...]
    unnamed x1 -> x6, local copies, waits for them, and re-layouts: 2.26 us -> 2.06 us
where the time goes in v3:
time: 83.6 us; the launch traced here: 83.4 us
  Pallas kernels  81.3 us (97%)
  local copies, waits for them, and re-layouts  2.06 us (2%)
    pallas_call x1, Pallas kernels, on_device(): pl.pallas_call(functools.partial(kernel, n, grp), out_shape=pltpu.VMEM((r...  80.3 us
    unnamed x6, local copies, waits for them, and re-layouts  2.06 us

profile of v3, /device:TPU:0, one launch (start us, length us, event | category | flops | bytes accessed | tf_op | source)
XLA Modules:
  0.0 83.4 jit_solution(7135709190672595426)
XLA Ops:
  0.0 0.0 copy-start
  0.0 0.7 copy-done
  0.7 0.0 copy-start.1
  0.7 0.7 copy-done.1
  1.4 0.0 copy-start.2
  1.4 0.7 copy-done.2
  2.1 80.3 %shard_map.73.in_ref = bf16[512,1024]{1,0:T(8,128)(2,1)S(1)} custom-call(s32[512]{0:T(512)S(1)} %copy-done.1, f32[1,128]{1,0:T(1,128)S(1)} %copy-done.2, f32[4608]{0:T(1024)S(1)} %copy-done, bf16[512,4608]{1,0:T(8,128)(2,1)} %tok_ref.1, bf16[2304,1024]{1,0:T(8,128)(2,1)} %q_ref.1, bf16[2304,512]{1,0:T(8,128)(2,1)} %k_ref.1, bf16[2304,512]{1,0:T(8,128)(2,1)} %v_ref.1), custom_call_target="tpu_custom_call" | custom-call | tf_op jit(solution)/shard_map/pallas_call | solution.py:328
  82.4 1.0 %shard_map.74 = bf16[512,1024]{1,0:T(8,128)(2,1)} custom-call(bf16[512,1024]{1,0:T(8,128)(2,1)S(1)} %shard_map.73.in_ref), custom_call_target="tpu_custom_call" | custom-call | tf_op jit(solution)/shard_map/pallas_call | solution.py:362
Async XLA Ops:
  0.0 0.7 copy-start
  0.7 0.7 copy-start.1
  1.4 0.7 copy-start.2
